TPU v7x, 128 devices: a whole 4x4x4 slice. The times are simulated.
128 devices in a mesh: seq: 16 (over x, y), head: 8 (over z, core).
Axes of the slice: x: 4, y: 4, z: 4, core: 2. Of those that a mesh axis runs over, the one named last changes fastest.
Arguments:
- queries: bfloat16 [4096, 12288], P('seq', 'head'), may hold values from -256 to 256
- own_latent: bfloat16 [4096, 576], P('seq'), may hold values from -16 to 16
- cache: bfloat16 [512, 128, 576], P('seq', 'head'), may hold values from -6 to 6
- block_list: int32 [16, 32], replicated, may hold values from 0 to 511, as said below
- offsets: int32 [16, 32], P('seq'), may hold values from -4096 to 4096
- tile_mask: int32 [16, 2, 32], P('seq'), may hold values 0 or 1
- w_uk: bfloat16 [64, 128, 512], P('head'), may hold values from -0.5 to 0.5
- w_uv: bfloat16 [64, 512, 128], P('head'), may hold values from -0.25 to 0.25
- w_o: bfloat16 [8192, 7168], P('head'), may hold values from -0.0625 to 0.0625
Outputs:
- layer_out: bfloat16 [4096, 7168], P('seq', 'head')
Inputs may be any that keep to these rules, and one draw needn't show every extreme that they name: `block_list`: entry (r, j) names a pooled span whose owner is index entry // 32 of seq. In each row no owner is named more than 4 times, and at least one owner is named exactly 4 times.
All inputs are finite; a program needn't handle non-finite values. No bound on the sum of `tile_mask` on one device may be relied on, other than what follows from the above.
Results may differ from a plain program's by a relative error of at most 0.015.
Values may be sent and summed in bfloat16 or wider, within the bound.
No kernel may reach another device: no remote copies, remote signals or barrier semaphores. Data moves between devices by JAX's collectives and lax.ppermute only.
A program may use at most 128 MiB of HBM per device.

v0:
```python
import jax
import jax.numpy as jnp
from jax import lax
from jax.sharding import PartitionSpec as P

MOST = 4
THETA = 50000.0


def rerotate(blocks, shift, latent_width):
    rotary_width = blocks.shape[-1] - latent_width
    halfway = rotary_width // 2
    inverse = THETA ** (-jnp.arange(halfway, dtype=jnp.float32) * 2.0 / rotary_width)
    angles = shift.astype(jnp.float32)[:, None] * inverse[None, :]
    cosine_table = jnp.cos(angles)[:, None, :]
    sine_table = jnp.sin(angles)[:, None, :]
    rotary = blocks[..., latent_width:].astype(jnp.float32)
    first_half = rotary[..., :halfway]
    second_half = rotary[..., halfway:]
    turned = jnp.concatenate(
        [
            first_half * cosine_table - second_half * sine_table,
            second_half * cosine_table + first_half * sine_table,
        ],
        axis=-1,
    )
    return jnp.concatenate([blocks[..., :latent_width], turned.astype(jnp.bfloat16)], axis=-1)


def allowed_keys(tiles, query_rows, block_rows):
    listed_mask = jnp.repeat(jnp.repeat(tiles > 0, block_rows, axis=0), block_rows, axis=1)
    causal = jnp.tril(jnp.ones((query_rows, query_rows), jnp.bool_))
    return jnp.concatenate([causal, listed_mask], axis=1)


def attend(grouped, context, allowed, key_maps, value_maps):
    nope_width = key_maps.shape[1]
    latent_width = key_maps.shape[2]
    factor = grouped.shape[-1] ** (-0.5)
    value_latent = context[:, :latent_width]

    def one_head(inputs):
        head_query, key_map, value_map = inputs
        query_latent = jnp.dot(
            head_query[:, :nope_width], key_map, preferred_element_type=jnp.float32
        ).astype(jnp.bfloat16)
        query_full = jnp.concatenate([query_latent, head_query[:, nope_width:]], axis=1)
        scores = (
            lax.dot_general(
                query_full, context, (((1,), (1,)), ((), ())), preferred_element_type=jnp.float32
            )
            * factor
        )
        scores = jnp.where(allowed, scores, -1e30)
        highest = jnp.max(scores, axis=1, keepdims=True)
        weights = jnp.exp(scores - highest)
        denominator = jnp.sum(weights, axis=1, keepdims=True)
        shares = (weights / denominator).astype(jnp.bfloat16)
        mixed_latent = jnp.dot(shares, value_latent, preferred_element_type=jnp.float32).astype(
            jnp.bfloat16
        )
        return jnp.dot(mixed_latent, value_map, preferred_element_type=jnp.float32).astype(
            jnp.bfloat16
        )

    per_head = lax.map(one_head, (jnp.transpose(grouped, (1, 0, 2)), key_maps, value_maps))
    return jnp.transpose(per_head, (1, 0, 2)).reshape(grouped.shape[0], -1)


def per_device(queries, own_latent, cache, block_list, offsets, tile_mask, w_uk, w_uv, w_o):
    seq_count = lax.axis_size("seq")
    seq_index = lax.axis_index("seq")
    spans_held = cache.shape[0]
    latent_full = cache.shape[2]
    listed_count = block_list.shape[1]
    owners = block_list // spans_held
    within = block_list % spans_held
    earlier = jnp.tril(jnp.ones((listed_count, listed_count), jnp.bool_), -1)
    same_owner = owners[:, :, None] == owners[:, None, :]
    ranking = jnp.sum(same_owner & earlier[None], axis=2)
    slot_ids = jnp.arange(MOST, dtype=jnp.int32)
    matches = (owners == seq_index)[:, :, None] & (ranking[:, :, None] == slot_ids[None, None, :])
    send_index = jnp.sum(jnp.where(matches, within[:, :, None], 0), axis=1)
    my_owners = lax.dynamic_index_in_dim(owners, seq_index, 0, keepdims=False)
    my_ranking = lax.dynamic_index_in_dim(ranking, seq_index, 0, keepdims=False)
    flat_slot = my_owners * MOST + my_ranking
    arrived = lax.all_to_all(cache[send_index], "seq", split_axis=0, concat_axis=0, tiled=True)
    picked = arrived.reshape(seq_count * MOST, cache.shape[1], latent_full)[flat_slot]
    blocks = lax.all_gather(picked, "head", axis=1, tiled=True)
    latent_width = w_uk.shape[2]
    block_rows = blocks.shape[1]
    turned = rerotate(blocks, offsets[0], latent_width).reshape(
        listed_count * block_rows, latent_full
    )
    context = jnp.concatenate([own_latent, turned], axis=0)
    query_rows = own_latent.shape[0]
    allowed = allowed_keys(tile_mask[0], query_rows, block_rows)
    head_width = w_uk.shape[1] + latent_full - latent_width
    grouped = queries.reshape(query_rows, -1, head_width)
    head_out = attend(grouped, context, allowed, w_uk, w_uv)
    partial_value = jnp.dot(head_out, w_o, preferred_element_type=jnp.float32)
    result = lax.psum_scatter(
        partial_value.astype(jnp.bfloat16), "head", scatter_dimension=1, tiled=True
    )
    return result


def solution(mesh):
    placed = (
        P("seq", "head"),
        P("seq", None),
        P("seq", "head", None),
        P(),
        P("seq", None),
        P("seq", None, None),
        P("head", None, None),
        P("head", None, None),
        P("head", None),
    )
    return jax.shard_map(
        per_device, mesh=mesh, in_specs=placed, out_specs=P("seq", "head"), check_vma=False
    )
```

profile of v0, /device:TPU:0, one launch (start us, length us, event | category | flops | bytes accessed | tf_op | source)
XLA Modules:
  0.0 265.0 jit_solution(6012045879321765092)
XLA Ops:
  10.7 7.3 %all-to-all-start = ((bf16[16,4,16,576]{3,2,1,0:T(8,128)(2,1)}), bf16[16,4,16,576]{3,2,1,0:T(8,128)(2,1)S(1)}, u32[]{:S(2)}, u32[]{:S(2)}) async-start(bf16[16,4,16,576]{3,2,1,0:T(8,128)(2,1)} %bitcast.7), calls=%async_computation | async-start | bytes 2621440 | tf_op jit(solution)/shard_map/all_to_all | solution.py:87
  18.1 20.7 %all-to-all-done = bf16[16,4,16,576]{3,2,1,0:T(8,128)(2,1)S(1)} async-done(((bf16[16,4,16,576]{3,2,1,0:T(8,128)(2,1)}), bf16[16,4,16,576]{3,2,1,0:T(8,128)(2,1)S(1)}, u32[]{:S(2)}, u32[]{:S(2)}) %all-to-all-start) | async-done | bytes 1179680 | tf_op jit(solution)/shard_map/all_to_all | solution.py:87
  45.4 30.7 %all-gather.3.cloned.1.call-done = bf16[32,128,576]{2,1,0:T(8,128)(2,1)} async-done(((bf16[32,16,576]{2,1,0:T(8,128)(2,1)}), bf16[32,128,576]{2,1,0:T(8,128)(2,1)}) %all-gather.3.cloned.1.call-update) | async-done | bytes 4718608 | tf_op jit(solution)/shard_map/all_gather | solution.py:89
  78.4 2.2 slice-done
  81.7 2.9 %pad_maximum_fusion = bf16[4352,576]{1,0:T(8,128)(2,1)} fusion(bf16[256,576]{1,0:T(8,128)(2,1)S(1)} %copy.24, bf16[4096,576]{1,0:T(8,128)(2,1)S(1)} %bitcast.53), kind=kLoop, calls=%fused_computation.28 | loop fusion | flops 10027008 | bytes 10027008 | tf_op jit(solution)/shard_map/concatenate | solution.py:95
  84.7 2.5 fusion.18
  87.1 115.0 %while.10 = (s32[]{:T(128)}, bf16[8,256,128]{1,2,0:T(8,128)(2,1)S(1)}, bf16[8,256,192]{1,2,0:T(8,128)(2,1)S(1)}, bf16[8,128,512]{2,1,0:T(8,128)(2,1)}, bf16[4352...) while((s32[]{:T(128)}, ...), condition=%wide.region_5.6_spmd, body=%wide.region_2.5_spmd.sunk | while | flops 2501213696 | bytes 43456640 | solution.py:66
  88.4 4.9 %fusion.41 = (f32[256]{0:T(256)S(1)}, f32[256,4352]{1,0:T(8,128)S(1)}) fusion(pred[256,4352]{1,0:T(32,128)(4,1)} %get-tuple-element.172, bf16[4352,576]{1,0:T(8,128)(2,1)} %get-tuple-element.171, bf16[256,64]{1,0:T(8,128)(2,1)S(1)} %slice.54, bf16[256,512]{1,0:T(8,128)(2,1)S(1)} %convolution_convert_fusion.3), kind=kOutput, calls=%fused_computation.63.clone.1 | convolution fusion | flops 1287388928 | bytes 10880000 | tf_op jit(solution)/shard_map/while/body/eval_jaxpr/dot_general | solution.py:49
  93.3 2.1 copy-done.2
  96.2 5.1 %fusion.43 = bf16[1,256,128]{2,1,0:T(8,128)(2,1)S(1)} fusion(bf16[4352,512]{1,0:T(8,128)(2,1)} %get-tuple-element.173, f32[256,4352]{1,0:T(8,128)} %copy-done.2, f32[256]{0:T(256)S(1)} %fusion.42, f32[256]{0:T(256)S(1)} %get-tuple-element.148, bf16[8,512,128]{2,1,0:T(8,128)(2,1)} %get-tuple-element.174, s32[]{:T(128)} %get-tuple-element.158), kind=kOutput, calls=%fused_computation.12.clone.1 | convolution fusion | flops 1177911296 | bytes 9112064 | tf_op jit(solution)/shard_map/while/body/eval_jaxpr/dot_general | solution.py:62
  102.8 4.9 %fusion.41 = (f32[256]{0:T(256)S(1)}, f32[256,4352]{1,0:T(8,128)S(1)}) fusion(pred[256,4352]{1,0:T(32,128)(4,1)} %get-tuple-element.172, bf16[4352,576]{1,0:T(8,128)(2,1)} %get-tuple-element.171, bf16[256,64]{1,0:T(8,128)(2,1)S(1)} %slice.54, bf16[256,512]{1,0:T(8,128)(2,1)S(1)} %convolution_convert_fusion.3), kind=kOutput, calls=%fused_computation.63.clone.1 | convolution fusion | flops 1287388928 | bytes 10880000 | tf_op jit(solution)/shard_map/while/body/eval_jaxpr/dot_general | solution.py:49
  107.7 2.1 copy-done.2
  110.6 5.1 %fusion.43 = bf16[1,256,128]{2,1,0:T(8,128)(2,1)S(1)} fusion(bf16[4352,512]{1,0:T(8,128)(2,1)} %get-tuple-element.173, f32[256,4352]{1,0:T(8,128)} %copy-done.2, f32[256]{0:T(256)S(1)} %fusion.42, f32[256]{0:T(256)S(1)} %get-tuple-element.148, bf16[8,512,128]{2,1,0:T(8,128)(2,1)} %get-tuple-element.174, s32[]{:T(128)} %get-tuple-element.158), kind=kOutput, calls=%fused_computation.12.clone.1 | convolution fusion | flops 1177911296 | bytes 9112064 | tf_op jit(solution)/shard_map/while/body/eval_jaxpr/dot_general | solution.py:62
  117.2 4.9 %fusion.41 = (f32[256]{0:T(256)S(1)}, f32[256,4352]{1,0:T(8,128)S(1)}) fusion(pred[256,4352]{1,0:T(32,128)(4,1)} %get-tuple-element.172, bf16[4352,576]{1,0:T(8,128)(2,1)} %get-tuple-element.171, bf16[256,64]{1,0:T(8,128)(2,1)S(1)} %slice.54, bf16[256,512]{1,0:T(8,128)(2,1)S(1)} %convolution_convert_fusion.3), kind=kOutput, calls=%fused_computation.63.clone.1 | convolution fusion | flops 1287388928 | bytes 10880000 | tf_op jit(solution)/shard_map/while/body/eval_jaxpr/dot_general | solution.py:49
  122.1 2.1 copy-done.2
  125.0 5.1 %fusion.43 = bf16[1,256,128]{2,1,0:T(8,128)(2,1)S(1)} fusion(bf16[4352,512]{1,0:T(8,128)(2,1)} %get-tuple-element.173, f32[256,4352]{1,0:T(8,128)} %copy-done.2, f32[256]{0:T(256)S(1)} %fusion.42, f32[256]{0:T(256)S(1)} %get-tuple-element.148, bf16[8,512,128]{2,1,0:T(8,128)(2,1)} %get-tuple-element.174, s32[]{:T(128)} %get-tuple-element.158), kind=kOutput, calls=%fused_computation.12.clone.1 | convolution fusion | flops 1177911296 | bytes 9112064 | tf_op jit(solution)/shard_map/while/body/eval_jaxpr/dot_general | solution.py:62
  131.5 4.9 %fusion.41 = (f32[256]{0:T(256)S(1)}, f32[256,4352]{1,0:T(8,128)S(1)}) fusion(pred[256,4352]{1,0:T(32,128)(4,1)} %get-tuple-element.172, bf16[4352,576]{1,0:T(8,128)(2,1)} %get-tuple-element.171, bf16[256,64]{1,0:T(8,128)(2,1)S(1)} %slice.54, bf16[256,512]{1,0:T(8,128)(2,1)S(1)} %convolution_convert_fusion.3), kind=kOutput, calls=%fused_computation.63.clone.1 | convolution fusion | flops 1287388928 | bytes 10880000 | tf_op jit(solution)/shard_map/while/body/eval_jaxpr/dot_general | solution.py:49
  136.5 2.1 copy-done.2
  139.4 5.1 %fusion.43 = bf16[1,256,128]{2,1,0:T(8,128)(2,1)S(1)} fusion(bf16[4352,512]{1,0:T(8,128)(2,1)} %get-tuple-element.173, f32[256,4352]{1,0:T(8,128)} %copy-done.2, f32[256]{0:T(256)S(1)} %fusion.42, f32[256]{0:T(256)S(1)} %get-tuple-element.148, bf16[8,512,128]{2,1,0:T(8,128)(2,1)} %get-tuple-element.174, s32[]{:T(128)} %get-tuple-element.158), kind=kOutput, calls=%fused_computation.12.clone.1 | convolution fusion | flops 1177911296 | bytes 9112064 | tf_op jit(solution)/shard_map/while/body/eval_jaxpr/dot_general | solution.py:62
  145.9 4.9 %fusion.41 = (f32[256]{0:T(256)S(1)}, f32[256,4352]{1,0:T(8,128)S(1)}) fusion(pred[256,4352]{1,0:T(32,128)(4,1)} %get-tuple-element.172, bf16[4352,576]{1,0:T(8,128)(2,1)} %get-tuple-element.171, bf16[256,64]{1,0:T(8,128)(2,1)S(1)} %slice.54, bf16[256,512]{1,0:T(8,128)(2,1)S(1)} %convolution_convert_fusion.3), kind=kOutput, calls=%fused_computation.63.clone.1 | convolution fusion | flops 1287388928 | bytes 10880000 | tf_op jit(solution)/shard_map/while/body/eval_jaxpr/dot_general | solution.py:49
  153.7 5.1 %fusion.43 = bf16[1,256,128]{2,1,0:T(8,128)(2,1)S(1)} fusion(bf16[4352,512]{1,0:T(8,128)(2,1)} %get-tuple-element.173, f32[256,4352]{1,0:T(8,128)} %copy-done.2, f32[256]{0:T(256)S(1)} %fusion.42, f32[256]{0:T(256)S(1)} %get-tuple-element.148, bf16[8,512,128]{2,1,0:T(8,128)(2,1)} %get-tuple-element.174, s32[]{:T(128)} %get-tuple-element.158), kind=kOutput, calls=%fused_computation.12.clone.1 | convolution fusion | flops 1177911296 | bytes 9112064 | tf_op jit(solution)/shard_map/while/body/eval_jaxpr/dot_general | solution.py:62
  160.3 4.9 %fusion.41 = (f32[256]{0:T(256)S(1)}, f32[256,4352]{1,0:T(8,128)S(1)}) fusion(pred[256,4352]{1,0:T(32,128)(4,1)} %get-tuple-element.172, bf16[4352,576]{1,0:T(8,128)(2,1)} %get-tuple-element.171, bf16[256,64]{1,0:T(8,128)(2,1)S(1)} %slice.54, bf16[256,512]{1,0:T(8,128)(2,1)S(1)} %convolution_convert_fusion.3), kind=kOutput, calls=%fused_computation.63.clone.1 | convolution fusion | flops 1287388928 | bytes 10880000 | tf_op jit(solution)/shard_map/while/body/eval_jaxpr/dot_general | solution.py:49
  165.3 2.1 copy-done.2
  168.1 5.1 %fusion.43 = bf16[1,256,128]{2,1,0:T(8,128)(2,1)S(1)} fusion(bf16[4352,512]{1,0:T(8,128)(2,1)} %get-tuple-element.173, f32[256,4352]{1,0:T(8,128)} %copy-done.2, f32[256]{0:T(256)S(1)} %fusion.42, f32[256]{0:T(256)S(1)} %get-tuple-element.148, bf16[8,512,128]{2,1,0:T(8,128)(2,1)} %get-tuple-element.174, s32[]{:T(128)} %get-tuple-element.158), kind=kOutput, calls=%fused_computation.12.clone.1 | convolution fusion | flops 1177911296 | bytes 9112064 | tf_op jit(solution)/shard_map/while/body/eval_jaxpr/dot_general | solution.py:62
  174.7 4.9 %fusion.41 = (f32[256]{0:T(256)S(1)}, f32[256,4352]{1,0:T(8,128)S(1)}) fusion(pred[256,4352]{1,0:T(32,128)(4,1)} %get-tuple-element.172, bf16[4352,576]{1,0:T(8,128)(2,1)} %get-tuple-element.171, bf16[256,64]{1,0:T(8,128)(2,1)S(1)} %slice.54, bf16[256,512]{1,0:T(8,128)(2,1)S(1)} %convolution_convert_fusion.3), kind=kOutput, calls=%fused_computation.63.clone.1 | convolution fusion | flops 1287388928 | bytes 10880000 | tf_op jit(solution)/shard_map/while/body/eval_jaxpr/dot_general | solution.py:49
  179.6 2.1 copy-done.2
  182.5 5.1 %fusion.43 = bf16[1,256,128]{2,1,0:T(8,128)(2,1)S(1)} fusion(bf16[4352,512]{1,0:T(8,128)(2,1)} %get-tuple-element.173, f32[256,4352]{1,0:T(8,128)} %copy-done.2, f32[256]{0:T(256)S(1)} %fusion.42, f32[256]{0:T(256)S(1)} %get-tuple-element.148, bf16[8,512,128]{2,1,0:T(8,128)(2,1)} %get-tuple-element.174, s32[]{:T(128)} %get-tuple-element.158), kind=kOutput, calls=%fused_computation.12.clone.1 | convolution fusion | flops 1177911296 | bytes 9112064 | tf_op jit(solution)/shard_map/while/body/eval_jaxpr/dot_general | solution.py:62
  189.1 4.9 %fusion.41 = (f32[256]{0:T(256)S(1)}, f32[256,4352]{1,0:T(8,128)S(1)}) fusion(pred[256,4352]{1,0:T(32,128)(4,1)} %get-tuple-element.172, bf16[4352,576]{1,0:T(8,128)(2,1)} %get-tuple-element.171, bf16[256,64]{1,0:T(8,128)(2,1)S(1)} %slice.54, bf16[256,512]{1,0:T(8,128)(2,1)S(1)} %convolution_convert_fusion.3), kind=kOutput, calls=%fused_computation.63.clone.1 | convolution fusion | flops 1287388928 | bytes 10880000 | tf_op jit(solution)/shard_map/while/body/eval_jaxpr/dot_general | solution.py:49
  196.9 5.1 %fusion.43 = bf16[1,256,128]{2,1,0:T(8,128)(2,1)S(1)} fusion(bf16[4352,512]{1,0:T(8,128)(2,1)} %get-tuple-element.173, f32[256,4352]{1,0:T(8,128)} %copy-done.2, f32[256]{0:T(256)S(1)} %fusion.42, f32[256]{0:T(256)S(1)} %get-tuple-element.148, bf16[8,512,128]{2,1,0:T(8,128)(2,1)} %get-tuple-element.174, s32[]{:T(128)} %get-tuple-element.158), kind=kOutput, calls=%fused_computation.12.clone.1 | convolution fusion | flops 1177911296 | bytes 9112064 | tf_op jit(solution)/shard_map/while/body/eval_jaxpr/dot_general | solution.py:62
  202.2 10.9 %convolution_convert_fusion.1 = bf16[256,7168]{1,0:T(8,128)(2,1)} fusion(bf16[256,1024]{0,1:T(8,128)(2,1)S(1)} %bitcast.62, bf16[1024,7168]{1,0:T(8,128)(2,1)} %param.19), kind=kOutput, calls=%fused_computation.26 | convolution fusion | flops 3759931392 | bytes 18874368 | tf_op jit(solution)/shard_map/dot_general | solution.py:101
  213.1 5.9 %copy.27 = bf16[256,7168]{0,1:T(8,128)(2,1)} copy(bf16[256,7168]{1,0:T(8,128)(2,1)} %convolution_convert_fusion.1) | data formatting | bytes 7340032
  219.0 37.2 %reduce-scatter.4.cloned.1.call-done = bf16[896,256]{1,0:T(8,128)(2,1)} async-done(((bf16[7168,256]{1,0:T(8,128)(2,1)}), bf16[896,256]{1,0:T(8,128)(2,1)}) %reduce-scatter.4.cloned.1.call-update) | async-done | bytes 458768
  (115 shorter events, 37.2 us)
Async XLA Ops:
  6.5 2.4 copy-start
  6.5 33.9 %copy-start.5 = (bf16[256,576]{0,1:T(8,128)(2,1)S(1)}, bf16[256,576]{0,1:T(8,128)(2,1)}, u32[]{:S(2)}) copy-start(bf16[256,576]{0,1:T(8,128)(2,1)} %param.12) | copy-start | bytes 884740
  6.5 34.1 %copy-start.6 = (s32[1,2,32]{2,1,0:T(2,128)S(1)}, s32[1,2,32]{2,1,0:T(2,128)}, u32[]{:S(2)}) copy-start(s32[1,2,32]{2,1,0:T(2,128)} %param.16) | copy-start | bytes 772
  10.7 32.7 %copy-start.3 = (bf16[256,1536]{1,0:T(8,128)(2,1)S(1)}, bf16[256,1536]{1,0:T(8,128)(2,1)}, u32[]{:S(2)}) copy-start(bf16[256,1536]{1,0:T(8,128)(2,1)} %param.11) | copy-start | bytes 2359300
  10.7 33.1 %copy-start.7 = (s32[1,32]{1,0:T(1,128)S(1)}, s32[1,32]{1,0:T(1,128)}, u32[]{:S(2)}) copy-start(s32[1,32]{1,0:T(1,128)} %param.15) | copy-start | bytes 388
  10.7 28.1 %all-to-all-start = ((bf16[16,4,16,576]{3,2,1,0:T(8,128)(2,1)}), bf16[16,4,16,576]{3,2,1,0:T(8,128)(2,1)S(1)}, u32[]{:S(2)}, u32[]{:S(2)}) async-start(bf16[16,4,16,576]{3,2,1,0:T(8,128)(2,1)} %bitcast.7), calls=%async_computation | async-start | bytes 2621440 | tf_op jit(solution)/shard_map/all_to_all | solution.py:87
  18.0 58.0 %all-gather.3.cloned.1.call-start = ((), (), s32[]{:S(2)}) async-start(), calls=%async_computation.2 | async-start | bytes 5898240 | tf_op jit(solution)/shard_map/all_gather | solution.py:89
  40.3 215.9 %reduce-scatter.4.cloned.1.call-start = ((), (), s32[]{:S(2)}) async-start(), calls=%async_computation.3 | async-start | bytes 4128768
  78.4 2.2 slice-start
  84.7 2.5 copy-start.4
  93.3 2.1 copy-start.2
  107.7 2.1 copy-start.2
  122.1 2.1 copy-start.2
  136.5 2.1 copy-start.2
  150.9 2.1 copy-start.2
  165.2 2.1 copy-start.2
  179.6 2.1 copy-start.2
  194.0 2.1 copy-start.2
  202.2 56.0 %copy-start.1 = (bf16[32,16,576]{2,1,0:T(8,128)(2,1)S(1)}, bf16[32,16,576]{2,1,0:T(8,128)(2,1)}, u32[]{:S(2)}) copy-start(bf16[32,16,576]{2,1,0:T(8,128)(2,1)} %param.13) | copy-start | bytes 1769476
Sparse Core Ops, SparseCore 0:
  40.5 35.5 all-gather.2
  219.1 37.0 reduce-scatter.3
where the time goes:
time: 266 us; the launch traced here: 265 us
  matrix products  100 us (38%)
  waiting for transfers between devices  88.6 us (33%)
  local copies, waits for them, and re-layouts  35.9 us (13%)
  other arithmetic  18.6 us (7%)
  between operations  13.6 us (5%)
  starting transfers between devices  7.36 us (3%)
    dot_general x8, matrix products, one_head(): jnp.dot(mixed_latent, value_map, preferred_element_type=jnp.float32)  41.1 us
    dot_general x8, matrix products, one_head(): lax.dot_general(query_full, context, (((1,), (1,)), ((), ())), preferred_...  39.5 us
    unnamed x3, waiting for transfers between devices  37.2 us
    all_gather x1, waiting for transfers between devices, per_device(): blocks = lax.all_gather(picked, 'head', axis=1, tiled=True)  30.7 us
    all_to_all x1, waiting for transfers between devices, per_device(): lax.all_to_all(cache[send_index], 'seq', split_axis=0, concat_axis=0, til...  20.7 us
    while x16, local copies, waits for them, and re-layouts  17.1 us
    dot_general x1, matrix products, per_device(): partial_value = jnp.dot(head_out, w_o, preferred_element_type=jnp.float32)  10.9 us
    unnamed x19, local copies, waits for them, and re-layouts  9.16 us
  transfers between devices with their start and end apart: 3, of which 3 were waited for; matrix products, arithmetic and copies ran while one was open for 2% of the time, Pallas kernels for 0%

commit v1 on v0

--- a/solution.py
+++ b/solution.py
@@ -86,7 +86,9 @@
     flat_slot = my_owners * MOST + my_ranking
     arrived = lax.all_to_all(cache[send_index], "seq", split_axis=0, concat_axis=0, tiled=True)
     picked = arrived.reshape(seq_count * MOST, cache.shape[1], latent_full)[flat_slot]
-    blocks = lax.all_gather(picked, "head", axis=1, tiled=True)
+    blocks = jnp.concatenate(
+        lax.all_to_all(jnp.stack([picked] * lax.axis_size("head")), "head", 0, 0), axis=1
+    )
     latent_width = w_uk.shape[2]
     block_rows = blocks.shape[1]
     turned = rerotate(blocks, offsets[0], latent_width).reshape(

time: 266 us -> 295 us (1.11)
  waiting for transfers between devices: 88.6 us -> 110 us
  starting transfers between devices: 7.36 us -> 12.6 us
  local copies, waits for them, and re-layouts: 35.9 us -> 39.3 us
    all_to_all x0 -> x1, waiting for transfers between devices: none -> 56 us  [per_device(): lax.all_to_all(jnp.stack([picked] * lax.axis_size('head')), 'head', 0, 0)]
    all_gather x1 -> x0, waiting for transfers between devices: 30.7 us -> none  [per_device(): blocks = lax.all_gather(picked, 'head', axis=1, tiled=True)]
    all_to_all x0 -> x1, starting transfers between devices: none -> 5.45 us  [per_device(): lax.all_to_all(jnp.stack([picked] * lax.axis_size('head')), 'head', 0, 0)]
    unnamed x3 -> x2, waiting for transfers between devices: 37.2 us -> 33.4 us
    reshape x0 -> x1, local copies, waits for them, and re-layouts: none -> 3.29 us  [per_device(): jnp.concatenate(lax.all_to_all(jnp.stack([picked] * lax.axis_size('head')...]
where the time goes in v1:
time: 295 us; the launch traced here: 294 us
  waiting for transfers between devices  110 us (37%)
  matrix products  101 us (34%)
  local copies, waits for them, and re-layouts  39.3 us (13%)
  other arithmetic  17.4 us (6%)
  between operations  13.6 us (5%)
  starting transfers between devices  12.6 us (4%)
    all_to_all x1, waiting for transfers between devices, per_device(): lax.all_to_all(jnp.stack([picked] * lax.axis_size('head')), 'head', 0, 0)  56 us
    dot_general x8, matrix products, one_head(): jnp.dot(mixed_latent, value_map, preferred_element_type=jnp.float32)  41.1 us
    dot_general x8, matrix products, one_head(): lax.dot_general(query_full, context, (((1,), (1,)), ((), ())), preferred_...  39.5 us
    unnamed x2, waiting for transfers between devices  33.4 us
    all_to_all x1, waiting for transfers between devices, per_device(): lax.all_to_all(cache[send_index], 'seq', split_axis=0, concat_axis=0, til...  20.8 us
    while x16, local copies, waits for them, and re-layouts  17.1 us
    dot_general x1, matrix products, per_device(): partial_value = jnp.dot(head_out, w_o, preferred_element_type=jnp.float32)  11 us
    unnamed x19, local copies, waits for them, and re-layouts  9.15 us
  transfers between devices with their start and end apart: 3, of which 3 were waited for; matrix products, arithmetic and copies ran while one was open for 2% of the time, Pallas kernels for 0%

profile of v1, /device:TPU:0, one launch (start us, length us, event | category | flops | bytes accessed | tf_op | source)
XLA Modules:
  0.0 294.2 jit_solution(3870206598032400949)
XLA Ops:
  10.7 7.1 %all-to-all-start = ((bf16[16,4,16,576]{3,2,1,0:T(8,128)(2,1)}), bf16[16,4,16,576]{3,2,1,0:T(8,128)(2,1)S(1)}, u32[]{:S(2)}, u32[]{:S(2)}) async-start(bf16[16,4,16,576]{3,2,1,0:T(8,128)(2,1)} %bitcast.7), calls=%async_computation | async-start | bytes 2621440 | tf_op jit(solution)/shard_map/all_to_all | solution.py:87
  17.9 20.8 %all-to-all-done = bf16[16,4,16,576]{3,2,1,0:T(8,128)(2,1)S(1)} async-done(((bf16[16,4,16,576]{3,2,1,0:T(8,128)(2,1)}), bf16[16,4,16,576]{3,2,1,0:T(8,128)(2,1)S(1)}, u32[]{:S(2)}, u32[]{:S(2)}) %all-to-all-start) | async-done | bytes 1179680 | tf_op jit(solution)/shard_map/all_to_all | solution.py:87
  39.3 2.8 stack.2
  42.1 5.4 %all-to-all-start.1 = ((bf16[8,32,16,576]{3,2,1,0:T(8,128)(2,1)}), bf16[8,32,16,576]{3,2,1,0:T(8,128)(2,1)}, u32[]{:S(2)}, u32[]{:S(2)}) async-start(bf16[8,32,16,576]{3,2,1,0:T(8,128)(2,1)} %stack.2), calls=%async_computation.1 | async-start | bytes 10485760 | tf_op jit(solution)/shard_map/all_to_all | solution.py:90
  52.5 56.0 %all-to-all-done.1 = bf16[8,32,16,576]{3,2,1,0:T(8,128)(2,1)} async-done(((bf16[8,32,16,576]{3,2,1,0:T(8,128)(2,1)}), bf16[8,32,16,576]{3,2,1,0:T(8,128)(2,1)}, u32[]{:S(2)}, u32[]{:S(2)}) %all-to-all-start.1) | async-done | bytes 4718624 | tf_op jit(solution)/shard_map/all_to_all | solution.py:90
  108.5 3.3 %copy.30 = bf16[32,8,16,576]{3,2,1,0:T(8,128)(2,1)S(1)} copy(bf16[32,8,16,576]{3,2,0,1:T(8,128)(2,1)} %bitcast.11) | data formatting | bytes 9437184 | tf_op jit(solution)/shard_map/reshape | solution.py:89
  114.5 3.0 %pad_maximum_fusion = bf16[4352,576]{1,0:T(8,128)(2,1)} fusion(bf16[256,576]{1,0:T(8,128)(2,1)S(1)} %copy.31, bf16[4096,576]{1,0:T(8,128)(2,1)S(1)} %bitcast.55), kind=kLoop, calls=%fused_computation.28 | loop fusion | flops 10027008 | bytes 10027008 | tf_op jit(solution)/shard_map/concatenate | solution.py:97
  117.5 2.5 fusion.18
  120.0 115.0 %while.10 = (s32[]{:T(128)}, bf16[8,256,128]{1,2,0:T(8,128)(2,1)S(1)}, bf16[8,256,192]{1,2,0:T(8,128)(2,1)S(1)}, bf16[8,128,512]{2,1,0:T(8,128)(2,1)}, bf16[4352...) while((s32[]{:T(128)}, ...), condition=%wide.region_5.6_spmd, body=%wide.region_2.5_spmd.sunk | while | flops 2501213696 | bytes 43456640 | solution.py:66
  121.2 4.9 %fusion.41 = (f32[256]{0:T(256)S(1)}, f32[256,4352]{1,0:T(8,128)S(1)}) fusion(pred[256,4352]{1,0:T(32,128)(4,1)} %get-tuple-element.180, bf16[4352,576]{1,0:T(8,128)(2,1)} %get-tuple-element.179, bf16[256,64]{1,0:T(8,128)(2,1)S(1)} %slice.54, bf16[256,512]{1,0:T(8,128)(2,1)S(1)} %convolution_convert_fusion.3), kind=kOutput, calls=%fused_computation.63.clone.1 | convolution fusion | flops 1287388928 | bytes 10880000 | tf_op jit(solution)/shard_map/while/body/eval_jaxpr/dot_general | solution.py:49
  126.2 2.1 copy-done.2
  129.0 5.1 %fusion.43 = bf16[1,256,128]{2,1,0:T(8,128)(2,1)S(1)} fusion(bf16[4352,512]{1,0:T(8,128)(2,1)} %get-tuple-element.181, f32[256,4352]{1,0:T(8,128)} %copy-done.2, f32[256]{0:T(256)S(1)} %fusion.42, f32[256]{0:T(256)S(1)} %get-tuple-element.156, bf16[8,512,128]{2,1,0:T(8,128)(2,1)} %get-tuple-element.182, s32[]{:T(128)} %get-tuple-element.166), kind=kOutput, calls=%fused_computation.12.clone.1 | convolution fusion | flops 1177911296 | bytes 9112064 | tf_op jit(solution)/shard_map/while/body/eval_jaxpr/dot_general | solution.py:62
  135.6 4.9 %fusion.41 = (f32[256]{0:T(256)S(1)}, f32[256,4352]{1,0:T(8,128)S(1)}) fusion(pred[256,4352]{1,0:T(32,128)(4,1)} %get-tuple-element.180, bf16[4352,576]{1,0:T(8,128)(2,1)} %get-tuple-element.179, bf16[256,64]{1,0:T(8,128)(2,1)S(1)} %slice.54, bf16[256,512]{1,0:T(8,128)(2,1)S(1)} %convolution_convert_fusion.3), kind=kOutput, calls=%fused_computation.63.clone.1 | convolution fusion | flops 1287388928 | bytes 10880000 | tf_op jit(solution)/shard_map/while/body/eval_jaxpr/dot_general | solution.py:49
  140.5 2.1 copy-done.2
  143.4 5.1 %fusion.43 = bf16[1,256,128]{2,1,0:T(8,128)(2,1)S(1)} fusion(bf16[4352,512]{1,0:T(8,128)(2,1)} %get-tuple-element.181, f32[256,4352]{1,0:T(8,128)} %copy-done.2, f32[256]{0:T(256)S(1)} %fusion.42, f32[256]{0:T(256)S(1)} %get-tuple-element.156, bf16[8,512,128]{2,1,0:T(8,128)(2,1)} %get-tuple-element.182, s32[]{:T(128)} %get-tuple-element.166), kind=kOutput, calls=%fused_computation.12.clone.1 | convolution fusion | flops 1177911296 | bytes 9112064 | tf_op jit(solution)/shard_map/while/body/eval_jaxpr/dot_general | solution.py:62
  150.0 4.9 %fusion.41 = (f32[256]{0:T(256)S(1)}, f32[256,4352]{1,0:T(8,128)S(1)}) fusion(pred[256,4352]{1,0:T(32,128)(4,1)} %get-tuple-element.180, bf16[4352,576]{1,0:T(8,128)(2,1)} %get-tuple-element.179, bf16[256,64]{1,0:T(8,128)(2,1)S(1)} %slice.54, bf16[256,512]{1,0:T(8,128)(2,1)S(1)} %convolution_convert_fusion.3), kind=kOutput, calls=%fused_computation.63.clone.1 | convolution fusion | flops 1287388928 | bytes 10880000 | tf_op jit(solution)/shard_map/while/body/eval_jaxpr/dot_general | solution.py:49
  154.9 2.1 copy-done.2
  157.8 5.1 %fusion.43 = bf16[1,256,128]{2,1,0:T(8,128)(2,1)S(1)} fusion(bf16[4352,512]{1,0:T(8,128)(2,1)} %get-tuple-element.181, f32[256,4352]{1,0:T(8,128)} %copy-done.2, f32[256]{0:T(256)S(1)} %fusion.42, f32[256]{0:T(256)S(1)} %get-tuple-element.156, bf16[8,512,128]{2,1,0:T(8,128)(2,1)} %get-tuple-element.182, s32[]{:T(128)} %get-tuple-element.166), kind=kOutput, calls=%fused_computation.12.clone.1 | convolution fusion | flops 1177911296 | bytes 9112064 | tf_op jit(solution)/shard_map/while/body/eval_jaxpr/dot_general | solution.py:62
  164.4 4.9 %fusion.41 = (f32[256]{0:T(256)S(1)}, f32[256,4352]{1,0:T(8,128)S(1)}) fusion(pred[256,4352]{1,0:T(32,128)(4,1)} %get-tuple-element.180, bf16[4352,576]{1,0:T(8,128)(2,1)} %get-tuple-element.179, bf16[256,64]{1,0:T(8,128)(2,1)S(1)} %slice.54, bf16[256,512]{1,0:T(8,128)(2,1)S(1)} %convolution_convert_fusion.3), kind=kOutput, calls=%fused_computation.63.clone.1 | convolution fusion | flops 1287388928 | bytes 10880000 | tf_op jit(solution)/shard_map/while/body/eval_jaxpr/dot_general | solution.py:49
  172.2 5.1 %fusion.43 = bf16[1,256,128]{2,1,0:T(8,128)(2,1)S(1)} fusion(bf16[4352,512]{1,0:T(8,128)(2,1)} %get-tuple-element.181, f32[256,4352]{1,0:T(8,128)} %copy-done.2, f32[256]{0:T(256)S(1)} %fusion.42, f32[256]{0:T(256)S(1)} %get-tuple-element.156, bf16[8,512,128]{2,1,0:T(8,128)(2,1)} %get-tuple-element.182, s32[]{:T(128)} %get-tuple-element.166), kind=kOutput, calls=%fused_computation.12.clone.1 | convolution fusion | flops 1177911296 | bytes 9112064 | tf_op jit(solution)/shard_map/while/body/eval_jaxpr/dot_general | solution.py:62
  178.7 4.9 %fusion.41 = (f32[256]{0:T(256)S(1)}, f32[256,4352]{1,0:T(8,128)S(1)}) fusion(pred[256,4352]{1,0:T(32,128)(4,1)} %get-tuple-element.180, bf16[4352,576]{1,0:T(8,128)(2,1)} %get-tuple-element.179, bf16[256,64]{1,0:T(8,128)(2,1)S(1)} %slice.54, bf16[256,512]{1,0:T(8,128)(2,1)S(1)} %convolution_convert_fusion.3), kind=kOutput, calls=%fused_computation.63.clone.1 | convolution fusion | flops 1287388928 | bytes 10880000 | tf_op jit(solution)/shard_map/while/body/eval_jaxpr/dot_general | solution.py:49
  183.7 2.1 copy-done.2
  186.6 5.1 %fusion.43 = bf16[1,256,128]{2,1,0:T(8,128)(2,1)S(1)} fusion(bf16[4352,512]{1,0:T(8,128)(2,1)} %get-tuple-element.181, f32[256,4352]{1,0:T(8,128)} %copy-done.2, f32[256]{0:T(256)S(1)} %fusion.42, f32[256]{0:T(256)S(1)} %get-tuple-element.156, bf16[8,512,128]{2,1,0:T(8,128)(2,1)} %get-tuple-element.182, s32[]{:T(128)} %get-tuple-element.166), kind=kOutput, calls=%fused_computation.12.clone.1 | convolution fusion | flops 1177911296 | bytes 9112064 | tf_op jit(solution)/shard_map/while/body/eval_jaxpr/dot_general | solution.py:62
  193.1 4.9 %fusion.41 = (f32[256]{0:T(256)S(1)}, f32[256,4352]{1,0:T(8,128)S(1)}) fusion(pred[256,4352]{1,0:T(32,128)(4,1)} %get-tuple-element.180, bf16[4352,576]{1,0:T(8,128)(2,1)} %get-tuple-element.179, bf16[256,64]{1,0:T(8,128)(2,1)S(1)} %slice.54, bf16[256,512]{1,0:T(8,128)(2,1)S(1)} %convolution_convert_fusion.3), kind=kOutput, calls=%fused_computation.63.clone.1 | convolution fusion | flops 1287388928 | bytes 10880000 | tf_op jit(solution)/shard_map/while/body/eval_jaxpr/dot_general | solution.py:49
  201.0 5.1 %fusion.43 = bf16[1,256,128]{2,1,0:T(8,128)(2,1)S(1)} fusion(bf16[4352,512]{1,0:T(8,128)(2,1)} %get-tuple-element.181, f32[256,4352]{1,0:T(8,128)} %copy-done.2, f32[256]{0:T(256)S(1)} %fusion.42, f32[256]{0:T(256)S(1)} %get-tuple-element.156, bf16[8,512,128]{2,1,0:T(8,128)(2,1)} %get-tuple-element.182, s32[]{:T(128)} %get-tuple-element.166), kind=kOutput, calls=%fused_computation.12.clone.1 | convolution fusion | flops 1177911296 | bytes 9112064 | tf_op jit(solution)/shard_map/while/body/eval_jaxpr/dot_general | solution.py:62
  207.5 4.9 %fusion.41 = (f32[256]{0:T(256)S(1)}, f32[256,4352]{1,0:T(8,128)S(1)}) fusion(pred[256,4352]{1,0:T(32,128)(4,1)} %get-tuple-element.180, bf16[4352,576]{1,0:T(8,128)(2,1)} %get-tuple-element.179, bf16[256,64]{1,0:T(8,128)(2,1)S(1)} %slice.54, bf16[256,512]{1,0:T(8,128)(2,1)S(1)} %convolution_convert_fusion.3), kind=kOutput, calls=%fused_computation.63.clone.1 | convolution fusion | flops 1287388928 | bytes 10880000 | tf_op jit(solution)/shard_map/while/body/eval_jaxpr/dot_general | solution.py:49
  215.3 5.1 %fusion.43 = bf16[1,256,128]{2,1,0:T(8,128)(2,1)S(1)} fusion(bf16[4352,512]{1,0:T(8,128)(2,1)} %get-tuple-element.181, f32[256,4352]{1,0:T(8,128)} %copy-done.2, f32[256]{0:T(256)S(1)} %fusion.42, f32[256]{0:T(256)S(1)} %get-tuple-element.156, bf16[8,512,128]{2,1,0:T(8,128)(2,1)} %get-tuple-element.182, s32[]{:T(128)} %get-tuple-element.166), kind=kOutput, calls=%fused_computation.12.clone.1 | convolution fusion | flops 1177911296 | bytes 9112064 | tf_op jit(solution)/shard_map/while/body/eval_jaxpr/dot_general | solution.py:62
  221.9 4.9 %fusion.41 = (f32[256]{0:T(256)S(1)}, f32[256,4352]{1,0:T(8,128)S(1)}) fusion(pred[256,4352]{1,0:T(32,128)(4,1)} %get-tuple-element.180, bf16[4352,576]{1,0:T(8,128)(2,1)} %get-tuple-element.179, bf16[256,64]{1,0:T(8,128)(2,1)S(1)} %slice.54, bf16[256,512]{1,0:T(8,128)(2,1)S(1)} %convolution_convert_fusion.3), kind=kOutput, calls=%fused_computation.63.clone.1 | convolution fusion | flops 1287388928 | bytes 10880000 | tf_op jit(solution)/shard_map/while/body/eval_jaxpr/dot_general | solution.py:49
  229.7 5.1 %fusion.43 = bf16[1,256,128]{2,1,0:T(8,128)(2,1)S(1)} fusion(bf16[4352,512]{1,0:T(8,128)(2,1)} %get-tuple-element.181, f32[256,4352]{1,0:T(8,128)} %copy-done.2, f32[256]{0:T(256)S(1)} %fusion.42, f32[256]{0:T(256)S(1)} %get-tuple-element.156, bf16[8,512,128]{2,1,0:T(8,128)(2,1)} %get-tuple-element.182, s32[]{:T(128)} %get-tuple-element.166), kind=kOutput, calls=%fused_computation.12.clone.1 | convolution fusion | flops 1177911296 | bytes 9112064 | tf_op jit(solution)/shard_map/while/body/eval_jaxpr/dot_general | solution.py:62
  235.0 11.0 %convolution_convert_fusion.1 = bf16[256,7168]{1,0:T(8,128)(2,1)} fusion(bf16[256,1024]{0,1:T(8,128)(2,1)S(1)} %bitcast.66, bf16[1024,7168]{1,0:T(8,128)(2,1)} %param.19), kind=kOutput, calls=%fused_computation.26 | convolution fusion | flops 3759931392 | bytes 18874368 | tf_op jit(solution)/shard_map/dot_general | solution.py:103
  246.0 5.9 %copy.34 = bf16[256,7168]{0,1:T(8,128)(2,1)} copy(bf16[256,7168]{1,0:T(8,128)(2,1)} %convolution_convert_fusion.1) | data formatting | bytes 7340032
  252.0 33.4 %reduce-scatter.4.cloned.1.call-done = bf16[896,256]{1,0:T(8,128)(2,1)} async-done(((bf16[7168,256]{1,0:T(8,128)(2,1)}), bf16[896,256]{1,0:T(8,128)(2,1)}) %reduce-scatter.4.cloned.1.call-update) | async-done | bytes 458768
  (115 shorter events, 39.8 us)
Async XLA Ops:
  6.5 2.4 copy-start
  10.7 27.9 %all-to-all-start = ((bf16[16,4,16,576]{3,2,1,0:T(8,128)(2,1)}), bf16[16,4,16,576]{3,2,1,0:T(8,128)(2,1)S(1)}, u32[]{:S(2)}, u32[]{:S(2)}) async-start(bf16[16,4,16,576]{3,2,1,0:T(8,128)(2,1)} %bitcast.7), calls=%async_computation | async-start | bytes 2621440 | tf_op jit(solution)/shard_map/all_to_all | solution.py:87
  42.1 5.5 %copy-start.5 = (bf16[256,576]{0,1:T(8,128)(2,1)S(1)}, bf16[256,576]{0,1:T(8,128)(2,1)}, u32[]{:S(2)}) copy-start(bf16[256,576]{0,1:T(8,128)(2,1)} %param.12) | copy-start | bytes 884740
  42.1 5.7 %copy-start.6 = (s32[1,2,32]{2,1,0:T(2,128)S(1)}, s32[1,2,32]{2,1,0:T(2,128)}, u32[]{:S(2)}) copy-start(s32[1,2,32]{2,1,0:T(2,128)} %param.16) | copy-start | bytes 772
  42.1 8.6 %copy-start.3 = (bf16[256,1536]{1,0:T(8,128)(2,1)S(1)}, bf16[256,1536]{1,0:T(8,128)(2,1)}, u32[]{:S(2)}) copy-start(bf16[256,1536]{1,0:T(8,128)(2,1)} %param.11) | copy-start | bytes 2359300
  42.1 66.4 %all-to-all-start.1 = ((bf16[8,32,16,576]{3,2,1,0:T(8,128)(2,1)}), bf16[8,32,16,576]{3,2,1,0:T(8,128)(2,1)}, u32[]{:S(2)}, u32[]{:S(2)}) async-start(bf16[8,32,16,576]{3,2,1,0:T(8,128)(2,1)} %stack.2), calls=%async_computation.1 | async-start | bytes 10485760 | tf_op jit(solution)/shard_map/all_to_all | solution.py:90
  47.5 3.5 %copy-start.7 = (s32[1,32]{1,0:T(1,128)S(1)}, s32[1,32]{1,0:T(1,128)}, u32[]{:S(2)}) copy-start(s32[1,32]{1,0:T(1,128)} %param.15) | copy-start | bytes 388
  47.5 237.8 %reduce-scatter.4.cloned.1.call-start = ((), (), s32[]{:S(2)}) async-start(), calls=%async_computation.3 | async-start | bytes 4128768
  117.5 2.5 copy-start.4
  126.2 2.1 copy-start.2
  140.5 2.1 copy-start.2
  154.9 2.1 copy-start.2
  169.3 2.1 copy-start.2
  183.7 2.1 copy-start.2
  198.1 2.1 copy-start.2
  212.5 2.1 copy-start.2
  226.8 2.1 copy-start.2
  235.0 52.3 %copy-start.1 = (bf16[32,16,576]{2,1,0:T(8,128)(2,1)S(1)}, bf16[32,16,576]{2,1,0:T(8,128)(2,1)}, u32[]{:S(2)}) copy-start(bf16[32,16,576]{2,1,0:T(8,128)(2,1)} %param.13) | copy-start | bytes 1769476
Sparse Core Ops, SparseCore 0:
  252.1 33.2 reduce-scatter.3
